TPU v7x, 256 devices: a whole 4x4x8 slice. The times are simulated.
256 devices in a mesh: batch: 128 (over x_hi, y, z, core), rep: 2 (over x_lo).
Axes of the slice: x: 4 (x_hi: 2, x_lo: 2; x = x_hi * 2 + x_lo), y: 4, z: 8, core: 2. Of those that a mesh axis runs over, the one named last changes fastest.
Arguments:
- image_embed: bfloat16 [16384, 1024], P('batch'), may hold values from -2 to 2
- text_embed: bfloat16 [16384, 1024], P(('batch', 'rep')), may hold values from -2 to 2
- logit_scale: float32 [1], replicated, may hold values from 50 to 100
Outputs:
- mean_loss: float32 [], replicated
- image_grad: float32 [16384, 1024], P(('batch', 'rep'))
- text_grad: float32 [16384, 1024], P(('batch', 'rep'))
All inputs are finite; a program needn't handle non-finite values.
Results may differ from a plain program's by a relative error of at most 0.0025.
Values may be sent and summed in bfloat16 or wider, within the bound.
No kernel may reach another device: no remote copies, remote signals or barrier semaphores. Data moves between devices by JAX's collectives and lax.ppermute only.
A program may use at most 128 MiB of HBM per device.

v0:
```python
import functools
import jax
import jax.numpy as jnp
from jax import lax
from jax.sharding import Mesh
from jax.sharding import PartitionSpec as P

BATCH = ("batch_0", "batch_1", "batch_2", "batch_3")
BATCH_REP = ("batch_0", "batch_1", "batch_2", "batch_3", "rep")


def copy_for_each(array, axis):
    peers = lax.axis_size(axis)
    return lax.all_to_all(
        jnp.broadcast_to(array[None], (peers, *array.shape)), axis, 0, 0, tiled=True
    )


def all_in_one(array, axis):
    leaves = jax.tree.leaves(array)
    sequence = sorted(range(len(leaves)), key=lambda k: -leaves[k].size)
    width = (1, *leaves[sequence[0]].shape)[-1]
    lines = [
        jnp.pad(leaves[k].reshape(-1), (0, -leaves[k].size % width)).reshape(-1, width)
        for k in sequence
    ]
    both, at, found = (copy_for_each(jnp.concatenate(lines), axis), 0, {})
    for k, line in zip(sequence, lines):
        share = both[:, at : at + len(line)].reshape(len(both), -1)
        found[k] = share[:, : leaves[k].size].reshape(-1, *leaves[k].shape)
        at += len(line)
    numbers = iter(range(len(leaves)))
    return jax.tree.map(lambda _: found[next(numbers)], array)


def joined_by_halves(pieces, combine):
    while len(jax.tree.leaves(pieces)[0]) > 1:
        pieces = jax.vmap(combine)(
            *(jax.tree.map(lambda part: part[side::2], pieces) for side in (0, 1))
        )
    return jax.tree.map(lambda part: part[0], pieces)


def merged(array, axis, combine):
    pieces = all_in_one(array, axis)
    return joined_by_halves(pieces, combine)


def collected_together(array, axis):
    leaves = jax.tree.leaves(array)
    sequence = sorted(range(len(leaves)), key=lambda k: -leaves[k].size)
    width = (1, *leaves[sequence[0]].shape)[-1]
    lines = [
        jnp.pad(leaves[k].reshape(-1), (0, -leaves[k].size % width)).reshape(-1, width)
        for k in sequence
    ]
    both, at, found = (lax.all_gather(jnp.concatenate(lines), axis), 0, {})
    for k, line in zip(sequence, lines):
        share = both[:, at : at + len(line)].reshape(len(both), -1)
        found[k] = share[:, : leaves[k].size].reshape(-1, *leaves[k].shape)
        at += len(line)
    numbers = iter(range(len(leaves)))
    return jax.tree.map(lambda _: found[next(numbers)], array)


def merged_by_axis(array, axes, combine):
    for axis in axes:
        pieces = collected_together(array, axis)
        array = jax.tree.map(lambda part: part[0], pieces)
        for k in range(1, lax.axis_size(axis)):
            array = combine(array, jax.tree.map(lambda part: part[k], pieces))
    return array


def over_axes(array, axes):
    return functools.reduce(lax.psum, axes, array)


def cut_along(array, dim, peers):
    lengths = array.shape
    parts = array.reshape(*lengths[:dim], peers, lengths[dim] // peers, *lengths[dim + 1 :])
    return jnp.moveaxis(parts, dim, 0)


def sum_at_owner(array, axis, dim):
    parts = cut_along(array, dim, lax.axis_size(axis))
    arrived = lax.all_to_all(parts, axis, split_axis=0, concat_axis=0, tiled=True)
    return arrived.sum(axis=0)


def combine_lse(earlier, later):
    biggest = jnp.maximum(earlier[0], later[0])
    return (
        biggest,
        earlier[1] * jnp.exp(earlier[0] - biggest) + later[1] * jnp.exp(later[0] - biggest),
    )


def body(image_embed, text_embed, logit_scale):
    scale_value = logit_scale[0]
    row_count = image_embed.shape[0]
    half_rows = text_embed.shape[0]
    batch_count = lax.axis_size(BATCH)
    batch_index = lax.axis_index(BATCH)
    rep_index = lax.axis_index("rep")
    whole_text = lax.all_gather(text_embed, BATCH, axis=0, tiled=True)
    scores = scale_value * lax.dot_general(
        image_embed, whole_text, (((1,), (1,)), ((), ())), preferred_element_type=jnp.float32
    )
    row_max = jnp.max(scores, axis=1)
    row_sum = jnp.sum(jnp.exp(scores - row_max[:, None]), axis=1)
    row_max, row_sum = merged((row_max, row_sum), "rep", combine_lse)
    row_lse = row_max + jnp.log(row_sum)
    column_max = jnp.max(scores, axis=0)
    column_sum = jnp.sum(jnp.exp(scores - column_max[None, :]), axis=0)
    column_max, column_sum = merged_by_axis((column_max, column_sum), BATCH, combine_lse)
    col_lse = column_max + jnp.log(column_sum)
    own_lse = lax.dynamic_slice_in_dim(col_lse, batch_index * half_rows, half_rows, 0)
    own_scores = lax.dynamic_slice(
        scores, (rep_index * half_rows, batch_index * half_rows), (half_rows, half_rows)
    )
    own_diag = jnp.diagonal(own_scores)
    own_rows = lax.dynamic_slice_in_dim(row_lse, rep_index * half_rows, half_rows, 0)
    loss_sum = over_axes(jnp.sum(own_rows + own_lse - 2.0 * own_diag), BATCH_REP)
    mean_loss = loss_sum / (2 * row_count * batch_count)
    row_ids = lax.broadcasted_iota(jnp.int32, scores.shape, 0) - rep_index * half_rows
    column_ids = lax.broadcasted_iota(jnp.int32, scores.shape, 1) - batch_index * half_rows
    diag_match = ((row_ids == column_ids) & (column_ids >= 0) & (column_ids < half_rows)).astype(
        jnp.float32
    )
    weights = (
        jnp.exp(scores - row_lse[:, None]) + jnp.exp(scores - col_lse[None, :]) - 2.0 * diag_match
    ).astype(jnp.bfloat16)
    image_part = (
        scale_value * 0.5 * jnp.dot(weights, whole_text, preferred_element_type=jnp.float32)
    )
    image_grad = sum_at_owner(image_part, "rep", 0)
    all_rows_lse = lax.all_gather(row_lse, BATCH, axis=0, tiled=True)
    own_first = (2 * batch_index + rep_index) * half_rows
    fragment = lax.all_gather(image_embed, BATCH, axis=0, tiled=True)
    scores_back = scale_value * lax.dot_general(
        text_embed, fragment, (((1,), (1,)), ((), ())), preferred_element_type=jnp.float32
    )
    image_ids = lax.broadcasted_iota(jnp.int32, scores_back.shape, 1)
    text_ids = own_first + lax.broadcasted_iota(jnp.int32, scores_back.shape, 0)
    back_match = (image_ids == text_ids).astype(jnp.float32)
    weights_block = (
        jnp.exp(scores_back - own_lse[:, None])
        + jnp.exp(scores_back - all_rows_lse[None, :])
        - 2.0 * back_match
    ).astype(jnp.bfloat16)
    summed = jnp.dot(weights_block, fragment, preferred_element_type=jnp.float32)
    text_grad = scale_value * 0.5 * summed
    return (mean_loss, image_grad, text_grad)


def solution(mesh):
    split = Mesh(
        mesh.devices.reshape(2, 4, 8, 2, mesh.shape["rep"]),
        ("batch_0", "batch_1", "batch_2", "batch_3", "rep"),
    )
    placed = (P(BATCH, None), P(BATCH_REP, None), P())
    return jax.shard_map(
        body,
        mesh=split,
        in_specs=placed,
        out_specs=(P(), P(BATCH_REP, None), P(BATCH_REP, None)),
        check_vma=False,
    )
```

profile of v0, /device:TPU:1, one launch (start us, length us, event | category | flops | bytes accessed | tf_op | source)
XLA Modules:
  0.0 527.8 jit_solution(11438516798877127760)
XLA Ops:
  7.2 0.0 all-gather.12.cloned.1.call-start
  7.2 0.7 all-gather.12.cloned.1.call-update
  7.9 0.0 all-gather.14.cloned.1.call-start
  7.9 0.7 all-gather.14.cloned.1.call-update
  9.4 157.7 %all-gather.12.cloned.1.call-done = bf16[8192,1024]{1,0:T(8,128)(2,1)} async-done(((bf16[64,1024]{1,0:T(8,128)(2,1)}), bf16[8192,1024]{1,0:T(8,128)(2,1)}) %all-gather.12.cloned.1.call-update) | async-done | bytes 16777232 | tf_op jit(solution)/shard_map/all_gather | solution.py:106
  167.1 13.5 %fusion.72 = (f32[128]{0:T(128)S(1)}, f32[8192]{0:T(1024)S(1)}, f32[128,8192]{1,0:T(8,128)}) fusion(bf16[128,1024]{1,0:T(8,128)(2,1)} %param.3, bf16[8192,1024]{1,0:T(8,128)(2,1)} %all-gather.12.cloned.1.call-done, f32[]{:T(128)} %bitcast.315), kind=kOutput, calls=%fused_computation.126 | convolution fusion | flops 2150621184 | bytes 21266948 | tf_op jit(solution)/shard_map/dot_general | solution.py:107
  180.7 3.6 exponential_reduce_fusion.1
  184.2 0.6 broadcast_in_dim.4
  184.8 3.2 all-to-all-start
  188.1 0.1 maximum_bitcast_fusion
  188.1 5.3 %all-gather.4 = f32[2,2,8192]{2,1,0:T(2,128)S(1)} all-gather(f32[1,2,8192]{2,1,0:T(2,128)S(1)} %maximum_bitcast_fusion), channel_id=2, replica_groups=mesh['batch_0'=2,'batch_1'=4,'batch_2'=8,'batch_3'=2,'rep'=2] {'batch_0'}, dimensions={0}, use_global_device_ids=true | all-gather | bytes 196608 | tf_op jit(solution)/shard_map/all_gather | solution.py:57
  193.4 0.1 fusion.47
  193.5 0.1 maximum_bitcast_fusion.1
  193.6 11.0 %all-gather.5 = f32[4,2,8192]{2,1,0:T(2,128)S(1)} all-gather(f32[1,2,8192]{2,1,0:T(2,128)S(1)} %maximum_bitcast_fusion.1), channel_id=3, replica_groups=mesh['batch_0'=2,'batch_1'=4,'batch_2'=8,'batch_3'=2,'rep'=2] {'batch_1'}, dimensions={0}, use_global_device_ids=true | all-gather | bytes 327680 | tf_op jit(solution)/shard_map/all_gather | solution.py:57
  204.6 0.3 fusion.38
  204.9 0.1 maximum_bitcast_fusion.2
  205.0 21.2 %all-gather.6 = f32[8,2,8192]{2,1,0:T(2,128)S(1)} all-gather(f32[1,2,8192]{2,1,0:T(2,128)S(1)} %maximum_bitcast_fusion.2), channel_id=4, replica_groups=mesh['batch_0'=2,'batch_1'=4,'batch_2'=8,'batch_3'=2,'rep'=2] {'batch_2'}, dimensions={0}, use_global_device_ids=true | all-gather | bytes 589824 | tf_op jit(solution)/shard_map/all_gather | solution.py:57
  226.2 0.7 fusion.17
  226.9 0.1 maximum_bitcast_fusion.3
  227.0 9.8 %all-gather.7 = f32[2,2,8192]{2,1,0:T(2,128)S(1)} all-gather(f32[1,2,8192]{2,1,0:T(2,128)S(1)} %maximum_bitcast_fusion.3), channel_id=5, replica_groups=mesh['batch_0'=2,'batch_1'=4,'batch_2'=8,'batch_3'=2,'rep'=2] {'batch_3'}, dimensions={0}, use_global_device_ids=true | all-gather | bytes 196608 | tf_op jit(solution)/shard_map/all_gather | solution.py:57
  236.8 0.1 fusion.76
  236.9 0.8 dynamic_slice.11
  237.8 0.8 gather_fusion
  238.6 0.0 all-to-all-done
  238.6 0.7 subtract_reduce_fusion
  239.3 5.9 %psum.35 = f32[]{:T(128)} all-reduce(f32[]{:T(128)} %get-tuple-element.7), channel_id=1, replica_groups=mesh['batch_0'=2,'batch_1'=4,'batch_2'=8,'batch_3'=2,'rep'=2] {'batch_0'}, use_global_device_ids=true, to_apply=%region_5.6 | all-reduce | flops 1 | bytes 8 | tf_op jit(solution)/shard_map/psum | solution.py:76
  245.2 9.5 %psum.36 = f32[]{:T(128)} all-reduce(f32[]{:T(128)} %psum.35), channel_id=1, replica_groups=mesh['batch_0'=2,'batch_1'=4,'batch_2'=8,'batch_3'=2,'rep'=2] {'batch_1'}, use_global_device_ids=true, to_apply=%region_6.7 | all-reduce | flops 1 | bytes 8 | tf_op jit(solution)/shard_map/psum | solution.py:76
  254.7 13.1 %psum.37 = f32[]{:T(128)} all-reduce(f32[]{:T(128)} %psum.36), channel_id=1, replica_groups=mesh['batch_0'=2,'batch_1'=4,'batch_2'=8,'batch_3'=2,'rep'=2] {'batch_2'}, use_global_device_ids=true, to_apply=%region_7.8 | all-reduce | flops 1 | bytes 8 | tf_op jit(solution)/shard_map/psum | solution.py:76
  267.8 9.0 %psum.38 = f32[]{:T(128)} all-reduce(f32[]{:T(128)} %psum.37), channel_id=1, replica_groups=mesh['batch_0'=2,'batch_1'=4,'batch_2'=8,'batch_3'=2,'rep'=2] {'batch_3'}, use_global_device_ids=true, to_apply=%region_8.9 | all-reduce | flops 1 | bytes 8 | tf_op jit(solution)/shard_map/psum | solution.py:76
  276.9 0.0 copy-start
  276.9 11.5 %fusion.14 = f32[128,1024]{1,0:T(8,128)} fusion(bf16[8192,1024]{1,0:T(8,128)(2,1)} %all-gather.12.cloned.1.call-done, f32[128,8192]{1,0:T(8,128)} %get-tuple-element.19, s32[8192]{0:T(1024)S(1)} %iota_subtract_fusion, f32[8192]{0:T(1024)S(1)} %log_add_fusion, f32[128]{0:T(128)S(1)} %log_add_fusion.1, s32[128]{0:T(128)S(1)} %iota_subtract_fusion.1, ...), kind=kOutput, calls=%fused_computation.22 | convolution fusion | flops 2157051904 | bytes 21578756 | tf_op jit(solution)/shard_map/dot_general | solution.py:135
  288.4 3.5 all-to-all-start.1
  291.9 15.4 %psum.39 = f32[]{:T(128)} all-reduce(f32[]{:T(128)} %psum.38), channel_id=1, replica_groups=mesh['batch_0'=2,'batch_1'=4,'batch_2'=8,'batch_3'=2,'rep'=2] {'rep'}, use_global_device_ids=true, to_apply=%region_9.10 | all-reduce | flops 1 | bytes 8 | tf_op jit(solution)/shard_map/psum | solution.py:76
  308.0 179.3 %all-gather.8 = f32[128,1,128]{2,1,0:T(1,128)S(1)} all-gather(f32[1,1,128]{2,1,0:T(1,128)S(1)} %fusion.83), channel_id=1, replica_groups=mesh['batch_0'=2,'batch_1'=4,'batch_2'=8,'batch_3'=2,'rep'=2] {'batch_0'..., dimensions={0}, use_global_device_ids=true | all-gather | bytes 66048 | tf_op jit(solution)/shard_map/all_gather | solution.py:138
  487.2 0.0 all-to-all-done.1
  487.2 0.7 reduce_sum.39
  488.0 0.0 all-gather.14.cloned.1.call-done
  488.0 0.0 copy-done
  488.0 31.9 %fusion.15 = f32[64,1024]{1,0:T(8,128)} fusion(bf16[16384,1024]{1,0:T(8,128)(2,1)} %all-gather.14.cloned.1.call-done, bf16[64,1024]{1,0:T(8,128)(2,1)S(1)} %copy-done, s32[64]{0:T(128)S(1)} %iota_add_fusion, f32[16384]{0:T(1024)S(1)} %bitcast.318, f32[64]{0:T(128)S(1)} %get-tuple-element.8, f32[]{:T(128)} %bitcast.317, f32[]{:T(128)S(6)} %mul.358), kind=kOutput, calls=%fused_computation.23 | convolution fusion | flops 4303421440 | bytes 34013704 | tf_op jit(solution)/shard_map/dot_general | solution.py:152
  (9 shorter events, 0.1 us)
Async XLA Ops:
  7.2 159.9 %all-gather.12.cloned.1.call-start = ((), (), s32[]{:S(2)}) async-start(), calls=%async_computation.2 | async-start | bytes 16908288 | tf_op jit(solution)/shard_map/all_gather | solution.py:106
  7.9 480.1 %all-gather.14.cloned.1.call-start = ((), (), s32[]{:S(2)}) async-start(), calls=%async_computation.3 | async-start | bytes 33816576 | tf_op jit(solution)/shard_map/all_gather | solution.py:140
  184.8 53.7 %all-to-all-start = ((f32[2,2,128]{2,1,0:T(2,128)}), f32[2,2,128]{2,1,0:T(2,128)S(1)}, u32[]{:S(2)}, u32[]{:S(2)}) async-start(f32[2,2,128]{2,1,0:T(2,128)} %broadcast_in_dim.4), calls=%async_computation | async-start | bytes 4096 | tf_op jit(solution)/shard_map/all_to_all | solution.py:14
  276.9 211.1 %copy-start = (bf16[64,1024]{1,0:T(8,128)(2,1)S(1)}, bf16[64,1024]{1,0:T(8,128)(2,1)}, u32[]{:S(2)}) copy-start(bf16[64,1024]{1,0:T(8,128)(2,1)} %param.4) | copy-start | bytes 393220
  288.4 198.9 %all-to-all-start.1 = ((f32[2,64,1024]{2,1,0:T(8,128)}), f32[2,64,1024]{2,1,0:T(8,128)S(1)}, u32[]{:S(2)}, u32[]{:S(2)}) async-start(f32[2,64,1024]{2,1,0:T(8,128)} %bitcast.46), calls=%async_computation.1 | async-start | bytes 1048576 | tf_op jit(solution)/shard_map/all_to_all | solution.py:87
Sparse Core Ops, SparseCore 0:
  11.6 155.4 all-gather.11
  170.7 214.5 all-gather.13
where the time goes:
time: 528 us
  blocking collectives  280 us (53%)
  waiting for transfers between devices  159 us (30%)
  matrix products  56.9 us (11%)
  between operations  16.6 us (3%)
  starting transfers between devices  6.79 us (1%)
  other arithmetic  6.55 us (1%)
    all_gather x1, blocking collectives, body(): all_rows_lse = lax.all_gather(row_lse, BATCH, axis=0, tiled=True)  179 us
    all_gather x1, waiting for transfers between devices, body(): whole_text = lax.all_gather(text_embed, BATCH, axis=0, tiled=True)  158 us
    psum x5, blocking collectives, over_axes(): return functools.reduce(lax.psum, axes, array)  53 us
    all_gather x4, blocking collectives, collected_together(): both, at, found = (lax.all_gather(jnp.concatenate(lines), axis), 0, {})  47.2 us
    dot_general x1, matrix products, body(): jnp.dot(weights_block, fragment, preferred_element_type=jnp.float32)  31.9 us
    dot_general x1, matrix products, body(): lax.dot_general(image_embed, whole_text, (((1,), (1,)), ((), ())), prefer...  13.5 us
    dot_general x1, matrix products, body(): jnp.dot(weights, whole_text, preferred_element_type=jnp.float32)  11.5 us
  transfers between devices with their start and end apart: 4, of which 1 were waited for; matrix products, arithmetic and copies ran while one was open for 6% of the time, Pallas kernels for 0%

commit v1 on v0

--- a/solution.py
+++ b/solution.py
@@ -103,7 +103,9 @@
     batch_count = lax.axis_size(BATCH)
     batch_index = lax.axis_index(BATCH)
     rep_index = lax.axis_index("rep")
-    whole_text = lax.all_gather(text_embed, BATCH, axis=0, tiled=True)
+    whole_text = jnp.concatenate(
+        lax.all_to_all(jnp.stack([text_embed] * lax.axis_size(BATCH)), BATCH, 0, 0), axis=0
+    )
     scores = scale_value * lax.dot_general(
         image_embed, whole_text, (((1,), (1,)), ((), ())), preferred_element_type=jnp.float32
     )

time: 528 us -> 836 us (1.58)
  waiting for transfers between devices: 159 us -> 451 us
  starting transfers between devices: 6.79 us -> 23.7 us
    all_to_all x0 -> x1, waiting for transfers between devices: none -> 450 us  [body(): lax.all_to_all(jnp.stack([text_embed] * lax.axis_size(BATCH)), BATCH, 0, 0)]
    all_gather x1 -> x0, waiting for transfers between devices: 158 us -> none  [body(): whole_text = lax.all_gather(text_embed, BATCH, axis=0, tiled=True)]
    all_to_all x0 -> x1, starting transfers between devices: none -> 17 us  [body(): lax.all_to_all(jnp.stack([text_embed] * lax.axis_size(BATCH)), BATCH, 0, 0)]
  transfers between devices with their start and end apart: 4 -> 4, of which waited for: 1 -> 1; matrix products, arithmetic and copies ran while one was open for 6% -> 5% of each run, Pallas kernels for 0% -> 0%
where the time goes in v1:
time: 836 us; the launch traced here: 835 us
  waiting for transfers between devices  451 us (54%)
  blocking collectives  272 us (33%)
  matrix products  56.8 us (7%)
  starting transfers between devices  23.7 us (3%)
  between operations  16.6 us (2%)
  local copies, waits for them, and re-layouts  9.04 us (1%)
    all_to_all x1, waiting for transfers between devices, body(): lax.all_to_all(jnp.stack([text_embed] * lax.axis_size(BATCH)), BATCH, 0, 0)  450 us
    all_gather x1, blocking collectives, body(): all_rows_lse = lax.all_gather(row_lse, BATCH, axis=0, tiled=True)  178 us
    all_gather x4, blocking collectives, collected_together(): both, at, found = (lax.all_gather(jnp.concatenate(lines), axis), 0, {})  48.4 us
    psum x5, blocking collectives, over_axes(): return functools.reduce(lax.psum, axes, array)  45.6 us
    dot_general x1, matrix products, body(): jnp.dot(weights_block, fragment, preferred_element_type=jnp.float32)  31.9 us
    all_to_all x1, starting transfers between devices, body(): lax.all_to_all(jnp.stack([text_embed] * lax.axis_size(BATCH)), BATCH, 0, 0)  17 us
  transfers between devices with their start and end apart: 4, of which 1 were waited for; matrix products, arithmetic and copies ran while one was open for 5% of the time, Pallas kernels for 0%

profile of v1, /device:TPU:1, one launch (start us, length us, event | category | flops | bytes accessed | tf_op | source)
XLA Modules:
  0.0 835.2 jit_solution(7280267484479434481)
XLA Ops:
  7.2 0.0 all-gather.11.cloned.1.call-start
  7.2 0.7 all-gather.11.cloned.1.call-update
  7.9 6.7 stack.2
  14.6 0.0 copy-start
  14.6 17.0 %all-to-all-start = ((bf16[128,64,1024]{2,1,0:T(8,128)(2,1)}), bf16[128,64,1024]{2,1,0:T(8,128)(2,1)}, u32[]{:S(2)}, u32[]{:S(2)}) async-start(bf16[128,64,1024]{2,1,0:T(8,128)(2,1)} %stack.2), calls=%async_computation | async-start | bytes 33554432 | tf_op jit(solution)/shard_map/all_to_all | solution.py:107
  32.3 450.0 %all-to-all-done = bf16[128,64,1024]{2,1,0:T(8,128)(2,1)} async-done(((bf16[128,64,1024]{2,1,0:T(8,128)(2,1)}), bf16[128,64,1024]{2,1,0:T(8,128)(2,1)}, u32[]{:S(2)}, u32[]{:S(2)}) %all-to-all-start) | async-done | bytes 16777248 | tf_op jit(solution)/shard_map/all_to_all | solution.py:107
  482.3 0.0 copy-done
  482.3 13.4 %fusion.72 = (f32[128]{0:T(128)S(1)}, f32[8192]{0:T(1024)S(1)}, f32[128,8192]{1,0:T(8,128)}) fusion(bf16[128,1024]{1,0:T(8,128)(2,1)S(1)} %copy-done, bf16[8192,1024]{1,0:T(8,128)(2,1)} %bitcast.1, f32[]{:T(128)} %bitcast.316), kind=kOutput, calls=%fused_computation.126 | convolution fusion | flops 2150621184 | bytes 21266948 | tf_op jit(solution)/shard_map/dot_general | solution.py:109
  495.7 3.5 exponential_reduce_fusion.1
  499.2 0.6 broadcast_in_dim.4
  499.8 3.2 all-to-all-start.1
  503.0 0.1 maximum_bitcast_fusion
  503.1 5.3 all-gather.4
  508.4 0.1 fusion.47
  508.5 0.1 maximum_bitcast_fusion.1
  508.6 9.8 %all-gather.5 = f32[4,2,8192]{2,1,0:T(2,128)S(1)} all-gather(f32[1,2,8192]{2,1,0:T(2,128)S(1)} %maximum_bitcast_fusion.1), channel_id=3, replica_groups=mesh['batch_0'=2,'batch_1'=4,'batch_2'=8,'batch_3'=2,'rep'=2] {'batch_1'}, dimensions={0}, use_global_device_ids=true | all-gather | bytes 327680 | tf_op jit(solution)/shard_map/all_gather | solution.py:57
  518.4 0.3 fusion.38
  518.7 0.1 maximum_bitcast_fusion.2
  518.8 21.6 %all-gather.6 = f32[8,2,8192]{2,1,0:T(2,128)S(1)} all-gather(f32[1,2,8192]{2,1,0:T(2,128)S(1)} %maximum_bitcast_fusion.2), channel_id=4, replica_groups=mesh['batch_0'=2,'batch_1'=4,'batch_2'=8,'batch_3'=2,'rep'=2] {'batch_2'}, dimensions={0}, use_global_device_ids=true | all-gather | bytes 589824 | tf_op jit(solution)/shard_map/all_gather | solution.py:57
  540.4 0.7 fusion.17
  541.1 0.1 maximum_bitcast_fusion.3
  541.2 11.7 %all-gather.7 = f32[2,2,8192]{2,1,0:T(2,128)S(1)} all-gather(f32[1,2,8192]{2,1,0:T(2,128)S(1)} %maximum_bitcast_fusion.3), channel_id=5, replica_groups=mesh['batch_0'=2,'batch_1'=4,'batch_2'=8,'batch_3'=2,'rep'=2] {'batch_3'}, dimensions={0}, use_global_device_ids=true | all-gather | bytes 196608 | tf_op jit(solution)/shard_map/all_gather | solution.py:57
  552.9 0.1 fusion.76
  553.0 0.8 dynamic_slice.11
  553.9 0.8 gather_fusion
  554.7 0.0 all-to-all-done.1
  554.7 0.7 subtract_reduce_fusion
  555.4 5.9 psum.35
  561.3 6.6 psum.36
  567.9 14.8 %psum.37 = f32[]{:T(128)} all-reduce(f32[]{:T(128)} %psum.36), channel_id=1, replica_groups=mesh['batch_0'=2,'batch_1'=4,'batch_2'=8,'batch_3'=2,'rep'=2] {'batch_2'}, use_global_device_ids=true, to_apply=%region_7.8 | all-reduce | flops 1 | bytes 8 | tf_op jit(solution)/shard_map/psum | solution.py:76
  582.7 9.6 %psum.38 = f32[]{:T(128)} all-reduce(f32[]{:T(128)} %psum.37), channel_id=1, replica_groups=mesh['batch_0'=2,'batch_1'=4,'batch_2'=8,'batch_3'=2,'rep'=2] {'batch_3'}, use_global_device_ids=true, to_apply=%region_8.9 | all-reduce | flops 1 | bytes 8 | tf_op jit(solution)/shard_map/psum | solution.py:76
  592.3 0.0 copy-start.1
  592.3 11.5 %fusion.14 = f32[128,1024]{1,0:T(8,128)} fusion(bf16[8192,1024]{1,0:T(8,128)(2,1)} %bitcast.1, f32[128,8192]{1,0:T(8,128)} %get-tuple-element.19, s32[8192]{0:T(1024)S(1)} %iota_subtract_fusion, f32[8192]{0:T(1024)S(1)} %log_add_fusion, f32[128]{0:T(128)S(1)} %log_add_fusion.1, s32[128]{0:T(128)S(1)} %iota_subtract_fusion.1, ...), kind=kOutput, calls=%fused_computation.22 | convolution fusion | flops 2157051904 | bytes 21578756 | tf_op jit(solution)/shard_map/dot_general | solution.py:137
  603.8 3.5 all-to-all-start.2
  607.3 8.7 %psum.39 = f32[]{:T(128)} all-reduce(f32[]{:T(128)} %psum.38), channel_id=1, replica_groups=mesh['batch_0'=2,'batch_1'=4,'batch_2'=8,'batch_3'=2,'rep'=2] {'rep'}, use_global_device_ids=true, to_apply=%region_9.10 | all-reduce | flops 1 | bytes 8 | tf_op jit(solution)/shard_map/psum | solution.py:76
  616.7 177.9 %all-gather.8 = f32[128,1,128]{2,1,0:T(1,128)S(1)} all-gather(f32[1,1,128]{2,1,0:T(1,128)S(1)} %fusion.83), channel_id=1, replica_groups=mesh['batch_0'=2,'batch_1'=4,'batch_2'=8,'batch_3'=2,'rep'=2] {'batch_0'..., dimensions={0}, use_global_device_ids=true | all-gather | bytes 66048 | tf_op jit(solution)/shard_map/all_gather | solution.py:140
  794.6 0.0 all-to-all-done.2
  794.6 0.7 reduce_sum.39
  795.4 0.0 all-gather.11.cloned.1.call-done
  795.4 0.0 copy-done.1
  795.4 31.9 %fusion.15 = f32[64,1024]{1,0:T(8,128)} fusion(bf16[16384,1024]{1,0:T(8,128)(2,1)} %all-gather.11.cloned.1.call-done, bf16[64,1024]{1,0:T(8,128)(2,1)S(1)} %copy-done.1, s32[64]{0:T(128)S(1)} %iota_add_fusion, f32[16384]{0:T(1024)S(1)} %bitcast.319, f32[64]{0:T(128)S(1)} %get-tuple-element.8, f32[]{:T(128)} %bitcast.318, f32[]{:T(128)S(6)} %mul.358), kind=kOutput, calls=%fused_computation.23 | convolution fusion | flops 4303421440 | bytes 34013704 | tf_op jit(solution)/shard_map/dot_general | solution.py:154
  (9 shorter events, 0.1 us)
Async XLA Ops:
  7.2 788.2 %all-gather.11.cloned.1.call-start = ((), (), s32[]{:S(2)}) async-start(), calls=%async_computation.3 | async-start | bytes 33816576 | tf_op jit(solution)/shard_map/all_gather | solution.py:142
  14.6 467.7 %copy-start = (bf16[128,1024]{1,0:T(8,128)(2,1)S(1)}, bf16[128,1024]{1,0:T(8,128)(2,1)}, u32[]{:S(2)}) copy-start(bf16[128,1024]{1,0:T(8,128)(2,1)} %param.3) | copy-start | bytes 786436
  14.6 467.7 %all-to-all-start = ((bf16[128,64,1024]{2,1,0:T(8,128)(2,1)}), bf16[128,64,1024]{2,1,0:T(8,128)(2,1)}, u32[]{:S(2)}, u32[]{:S(2)}) async-start(bf16[128,64,1024]{2,1,0:T(8,128)(2,1)} %stack.2), calls=%async_computation | async-start | bytes 33554432 | tf_op jit(solution)/shard_map/all_to_all | solution.py:107
  499.8 54.9 %all-to-all-start.1 = ((f32[2,2,128]{2,1,0:T(2,128)}), f32[2,2,128]{2,1,0:T(2,128)S(1)}, u32[]{:S(2)}, u32[]{:S(2)}) async-start(f32[2,2,128]{2,1,0:T(2,128)} %broadcast_in_dim.4), calls=%async_computation.1 | async-start | bytes 4096 | tf_op jit(solution)/shard_map/all_to_all | solution.py:14
  592.3 203.1 %copy-start.1 = (bf16[64,1024]{1,0:T(8,128)(2,1)S(1)}, bf16[64,1024]{1,0:T(8,128)(2,1)}, u32[]{:S(2)}) copy-start(bf16[64,1024]{1,0:T(8,128)(2,1)} %param.4) | copy-start | bytes 393220
  603.8 190.9 %all-to-all-start.2 = ((f32[2,64,1024]{2,1,0:T(8,128)}), f32[2,64,1024]{2,1,0:T(8,128)S(1)}, u32[]{:S(2)}, u32[]{:S(2)}) async-start(f32[2,64,1024]{2,1,0:T(8,128)} %bitcast.47), calls=%async_computation.2 | async-start | bytes 1048576 | tf_op jit(solution)/shard_map/all_to_all | solution.py:87
Sparse Core Ops, SparseCore 0:
  11.6 454.2 all-gather.10
